TPU v7x, 256 devices: a whole 4x4x8 slice. The times are simulated.
256 devices in a mesh: rows: 32 (over z, y_lo, core), cols: 8 (over x, y_hi).
Axes of the slice: x: 4, y: 4 (y_hi: 2, y_lo: 2; y = y_hi * 2 + y_lo), z: 8, core: 2. Of those that a mesh axis runs over, the one named last changes fastest.
Arguments:
- matrix: float32 [8192, 8192], P('rows', 'cols'), may hold values from -6 to 6
- starts: int32 [4, 4], replicated, may hold values from 0 to 7936, as said below
- factors: float32 [4, 4, 256, 256], P(None, None, 'rows', 'cols'), as said below
Outputs:
- updated: float32 [8192, 8192], P('rows', 'cols')
Inputs may be any that keep to these rules, and one draw needn't show every extreme that they name: `starts`: every start is a multiple of 128; chain c's start lies in the c-th of 4 equal ranges of blocks and never decreases from advance to advance; a window may end on the first block of the next range; the windows of one advance are disjoint. `factors`: every factor is orthogonal.
All inputs are finite; a program needn't handle non-finite values.
Results may differ from a plain program's by a relative error of at most 0.0001.
Values sent between devices are 32-bit elements; how exact they have to be, the bound alone decides.
No kernel may reach another device: no remote copies, remote signals or barrier semaphores. Data moves between devices by JAX's collectives and lax.ppermute only.
A program may use at most 64 MiB of HBM per device.

v0:
```python
import jax
import jax.numpy as jnp
from jax import lax
from jax.sharding import Mesh
from jax.sharding import PartitionSpec as P

NB = 128
CHAINS = 4
ADV = 4
COLS = ("cols_0", "cols_1")


def joined_along(tiles, dim):
    tiles = jnp.moveaxis(tiles, 0, dim)
    dims = tiles.shape
    return tiles.reshape(*dims[:dim], dims[dim] * dims[dim + 1], *dims[dim + 2 :])


def sent_to_all(x, axis):
    length = lax.axis_size(axis)
    return lax.all_to_all(jnp.broadcast_to(x[None], (length, *x.shape)), axis, 0, 0, tiled=True)


def gathered_copies(x, axis, dim):
    return joined_along(sent_to_all(x, axis), dim)


def gather_axes(x, axes, dim):
    for axis in reversed(axes):
        x = lax.all_gather(x, axis, axis=dim, tiled=True)
    return x


def from_behind(value, axis, steps):
    count = lax.axis_size(axis)
    pairs = [(source, (source + steps) % count) for source in range(count)]
    return lax.ppermute(value, axis, pairs)


def owned_blocks(matrix_tile, block_ids, position, devices, dimension):
    portions = []
    places = []
    for block_id in block_ids:
        owner_id = block_id % devices
        slot_id = block_id // devices
        portion = lax.dynamic_slice_in_dim(matrix_tile, slot_id * NB, NB, dimension)
        is_owner = owner_id == position
        portions.append(jnp.where(is_owner, portion, jnp.zeros_like(portion)))
        places.append((slot_id, is_owner))
    return (jnp.stack(portions), places)


def write_block(matrix_tile, new_portion, place, dimension):
    slot_id, is_owner = place
    current = lax.dynamic_slice_in_dim(matrix_tile, slot_id * NB, NB, dimension)
    chosen = jnp.where(is_owner, new_portion, current)
    return lax.dynamic_update_slice_in_dim(matrix_tile, chosen, slot_id * NB, dimension)


def local(matrix, starts, factors):
    row_devices = lax.axis_size("rows")
    row_position = lax.axis_index("rows")
    col_devices = lax.axis_size(COLS)
    col_position = lax.axis_index(COLS)
    matrix_tile = matrix
    whole_factors = gathered_copies(factors, "rows", 2)
    whole_factors = gather_axes(whole_factors, COLS, 3)
    for advance in range(ADV):
        advance_factors = whole_factors[advance]
        window_heads = [starts[advance, chain_id] // NB for chain_id in range(CHAINS)]
        window_tails = [head_id + 1 for head_id in window_heads]
        first_rows, first_places = owned_blocks(
            matrix_tile, window_heads, row_position, row_devices, 0
        )
        second_rows, second_places = owned_blocks(
            matrix_tile, window_tails, row_position, row_devices, 0
        )
        got_first = from_behind(first_rows, "rows", 1)
        got_second = from_behind(second_rows, "rows", -1)
        window = jnp.concatenate([first_rows + got_first, second_rows + got_second], axis=1)
        changed = jnp.einsum(
            "cji,cjk->cik",
            advance_factors,
            window,
            precision=lax.Precision.HIGHEST,
            preferred_element_type=jnp.float32,
        )
        for chain_id in range(CHAINS):
            matrix_tile = write_block(
                matrix_tile, changed[chain_id, :NB], first_places[chain_id], 0
            )
            matrix_tile = write_block(
                matrix_tile, changed[chain_id, NB:], second_places[chain_id], 0
            )
        first_cols, first_spots = owned_blocks(
            matrix_tile, window_heads, col_position, col_devices, 1
        )
        second_cols, second_spots = owned_blocks(
            matrix_tile, window_tails, col_position, col_devices, 1
        )
        got_left = from_behind(first_cols, COLS, 1)
        got_right = from_behind(second_cols, COLS, -1)
        column_window = jnp.concatenate([first_cols + got_left, second_cols + got_right], axis=2)
        turned = jnp.einsum(
            "crj,cji->cri",
            column_window,
            advance_factors,
            precision=lax.Precision.HIGHEST,
            preferred_element_type=jnp.float32,
        )
        for chain_id in range(CHAINS):
            matrix_tile = write_block(
                matrix_tile, turned[chain_id, :, :NB], first_spots[chain_id], 1
            )
            matrix_tile = write_block(
                matrix_tile, turned[chain_id, :, NB:], second_spots[chain_id], 1
            )
    return matrix_tile


def solution(mesh):
    finer = Mesh(mesh.devices.reshape(mesh.shape["rows"], 4, 2), ("rows", "cols_0", "cols_1"))
    in_specs = (P("rows", COLS), P(), P(None, None, "rows", COLS))
    out_specs = P("rows", COLS)
    return jax.shard_map(local, mesh=finer, in_specs=in_specs, out_specs=out_specs, check_vma=False)
```

profile of v0, /device:TPU:72, one launch (start us, length us, event | category | flops | bytes accessed | tf_op | source)
XLA Modules:
  0.0 458.1 jit_solution(5475957764767053818)
XLA Ops:
  8.6 24.4 %all_to_all.5 = f32[32,1,4096]{2,1,0:T(1,128)S(1)} all-to-all(f32[32,1,4096]{2,1,0:T(1,128)S(1)} %reshape.5), channel_id=1, replica_groups=mesh['rows'=32,'cols_0'=4,'cols_1'=2] {'rows'}, dimensions={0} | all-to-all | bytes 1048576 | tf_op jit(solution)/shard_map/all_to_all | solution.py:21
  33.5 1.9 reduce
  36.1 1.6 copy_bitcast_fusion
  37.7 3.1 copy.109
  40.9 26.1 %all-gather.3.cloned.1.call-done = f32[4,4,256,64]{2,1,0,3:T(4,128)} async-done(((f32[4,4,256,32]{2,1,0,3:T(4,128)}), f32[4,4,256,64]{2,1,0,3:T(4,128)}) %all-gather.3.cloned.1.call-update) | async-done | bytes 1048592 | tf_op jit(solution)/shard_map/all_gather | solution.py:30
  78.9 1.6 pad_maximum_fusion
  82.3 2.2 collective-permute-start.1
  84.5 44.6 %collective-permute-done = f32[4,128,1024]{1,2,0:T(8,128)} collective-permute-done((f32[4,128,1024]{1,2,0:T(8,128)}, f32[4,128,1024]{1,2,0:T(8,128)}, u32[]{:S(2)}, u32[]{:S(2)}) %collective-permute-start) | collective-permute-done | bytes 2097184 | tf_op jit(solution)/shard_map/ppermute | solution.py:37
  129.1 3.7 fusion.203
  132.8 3.1 fusion.202
  136.0 4.3 fusion.204
  140.7 5.5 %fusion.25 = f32[4,256,1024]{1,2,0:T(8,128)S(1)} fusion(f32[4,128,1024]{1,2,0:T(8,128)} %fusion.202, f32[4,128,1024]{1,2,0:T(8,128)} %fusion.203, f32[1,4,256,256]{3,2,1,0:T(8,128)S(1)} %copy.160), kind=kOutput, calls=%fused_computation.19 | convolution fusion | flops 3222274048 | bytes 9437184 | tf_op jit(solution)/shard_map/cji,cjk->cik/dot_general | solution.py:81
  150.3 4.2 collective-permute-start.3
  164.9 19.6 %collective-permute-done.2 = f32[4,256,128]{1,2,0:T(8,128)} collective-permute-done((f32[4,256,128]{1,2,0:T(8,128)}, f32[4,256,128]{1,2,0:T(8,128)}, u32[]{:S(2)}, u32[]{:S(2)}) %collective-permute-start.2) | collective-permute-done | bytes 524320 | tf_op jit(solution)/shard_map/ppermute | solution.py:37
  185.7 3.6 collective-permute-done.3
  190.3 1.9 fusion.28
  192.9 1.6 pad_maximum_fusion.2
  195.1 1.5 pad_maximum_fusion.3
  196.6 1.6 collective-permute-start.5
  198.2 1.6 copy.161
  199.8 32.0 %collective-permute-done.4 = f32[4,128,1024]{1,2,0:T(8,128)} collective-permute-done((f32[4,128,1024]{1,2,0:T(8,128)}, f32[4,128,1024]{1,2,0:T(8,128)}, u32[]{:S(2)}, u32[]{:S(2)}) %collective-permute-start.4) | collective-permute-done | bytes 2097184 | tf_op jit(solution)/shard_map/ppermute | solution.py:37
  231.8 2.4 fusion.201
  234.2 1.9 fusion.200
  236.1 3.8 fusion.22
  242.7 5.6 %collective-permute-start.7 = (f32[4,256,128]{1,2,0:T(8,128)}, f32[4,256,128]{1,2,0:T(8,128)}, u32[]{:S(2)}, u32[]{:S(2)}) collective-permute-start(f32[4,256,128]{1,2,0:T(8,128)} %pad_maximum_fusion.11), channel_id=1, source_target_pairs={{0,7},{1,0},{2,1},{3,2},{4,3},{5,4},{6,5},{7,6},{8,15},{9,8},{10,9... | collective-permute-start | bytes 1572872 | tf_op jit(solution)/shard_map/ppermute | solution.py:37
  258.2 15.7 %collective-permute-done.6 = f32[4,256,128]{1,2,0:T(8,128)} collective-permute-done((f32[4,256,128]{1,2,0:T(8,128)}, f32[4,256,128]{1,2,0:T(8,128)}, u32[]{:S(2)}, u32[]{:S(2)}) %collective-permute-start.6) | collective-permute-done | bytes 524320 | tf_op jit(solution)/shard_map/ppermute | solution.py:37
  276.6 1.9 fusion.32
  279.1 1.6 pad_maximum_fusion.4
  282.9 1.6 collective-permute-start.9
  284.5 1.6 copy.162
  286.1 40.5 %collective-permute-done.8 = f32[4,128,1024]{1,2,0:T(8,128)} collective-permute-done((f32[4,128,1024]{1,2,0:T(8,128)}, f32[4,128,1024]{1,2,0:T(8,128)}, u32[]{:S(2)}, u32[]{:S(2)}) %collective-permute-start.8) | collective-permute-done | bytes 2097184 | tf_op jit(solution)/shard_map/ppermute | solution.py:37
  326.6 2.4 fusion.199
  329.0 1.9 fusion.198
  330.9 3.8 fusion.19
  337.7 5.4 %collective-permute-start.11 = (f32[4,256,128]{1,2,0:T(8,128)}, f32[4,256,128]{1,2,0:T(8,128)}, u32[]{:S(2)}, u32[]{:S(2)}) collective-permute-start(f32[4,256,128]{1,2,0:T(8,128)} %pad_maximum_fusion.13), channel_id=1, source_target_pairs={{0,7},{1,0},{2,1},{3,2},{4,3},{5,4},{6,5},{7,6},{8,15},{9,8},{10,9... | collective-permute-start | bytes 1572872 | tf_op jit(solution)/shard_map/ppermute | solution.py:37
  353.5 11.1 %collective-permute-done.10 = f32[4,256,128]{1,2,0:T(8,128)} collective-permute-done((f32[4,256,128]{1,2,0:T(8,128)}, f32[4,256,128]{1,2,0:T(8,128)}, u32[]{:S(2)}, u32[]{:S(2)}) %collective-permute-start.10) | collective-permute-done | bytes 524320 | tf_op jit(solution)/shard_map/ppermute | solution.py:37
  366.8 1.9 fusion.36
  369.3 1.6 pad_maximum_fusion.6
  373.1 1.6 collective-permute-start.13
  374.7 1.6 copy.163
  376.3 45.2 %collective-permute-done.12 = f32[4,128,1024]{1,2,0:T(8,128)} collective-permute-done((f32[4,128,1024]{1,2,0:T(8,128)}, f32[4,128,1024]{1,2,0:T(8,128)}, u32[]{:S(2)}, u32[]{:S(2)}) %collective-permute-start.12) | collective-permute-done | bytes 2097184 | tf_op jit(solution)/shard_map/ppermute | solution.py:37
  421.6 2.4 fusion.197
  424.0 1.9 fusion.196
  425.9 3.8 fusion.16
  430.9 5.7 %collective-permute-start.15 = (f32[4,256,128]{1,2,0:T(8,128)S(1)}, f32[4,256,128]{1,2,0:T(8,128)S(1)}, u32[]{:S(2)}, u32[]{:S(2)}) collective-permute-start(f32[4,256,128]{1,2,0:T(8,128)S(1)} %pad_maximum_fusion.15), channel_id=1, source_target_pairs={{0,7},{1,0},{2,1},{3,2},{4,3},{5,4},{6,5},{7,6},{8,15},{9,8},{10,9... | collective-permute-start | bytes 1572872 | tf_op jit(solution)/shard_map/ppermute | solution.py:37
  436.6 7.1 %collective-permute-done.14 = f32[4,256,128]{1,2,0:T(8,128)S(1)} collective-permute-done((f32[4,256,128]{1,2,0:T(8,128)S(1)}, f32[4,256,128]{1,2,0:T(8,128)S(1)}, u32[]{:S(2)}, u32[]{:S(2)}) %collective-permute-start.14) | collective-permute-done | bytes 524320 | tf_op jit(solution)/shard_map/ppermute | solution.py:37
  443.8 3.5 collective-permute-done.15
  447.4 1.9 fusion.40
  (178 shorter events, 33.0 us)
Async XLA Ops:
  6.5 60.5 %all-gather.3.cloned.1.call-start = ((), (), s32[]{:S(2)}) async-start(), calls=%async_computation.1 | async-start | bytes 1572864 | tf_op jit(solution)/shard_map/all_gather | solution.py:30
  37.7 29.4 %copy-start.29 = (s32[4,4]{1,0:T(4,128)S(1)}, s32[4,4]{1,0:T(4,128)}, u32[]{:S(2)}) copy-start(s32[4,4]{1,0:T(4,128)} %param.4) | copy-start | bytes 196
  37.7 40.5 %copy-start.28 = (f32[256,1024]{1,0:T(8,128)S(1)}, f32[256,1024]{1,0:T(8,128)}, u32[]{:S(2)}) copy-start(f32[256,1024]{1,0:T(8,128)} %param.3) | copy-start | bytes 3145732
  40.8 95.1 %all-gather.5.cloned.1.call-start = ((), (), s32[]{:S(2)}) async-start(), calls=%async_computation.2 | async-start | bytes 5242880 | tf_op jit(solution)/shard_map/all_gather | solution.py:30
  78.9 1.7 copy-start
  78.9 1.7 copy-start.1
  78.9 1.8 copy-start.2
  78.9 2.0 copy-start.3
  80.9 48.2 %collective-permute-start = (f32[4,128,1024]{1,2,0:T(8,128)}, f32[4,128,1024]{1,2,0:T(8,128)}, u32[]{:S(2)}, u32[]{:S(2)}) collective-permute-start(f32[4,128,1024]{1,2,0:T(8,128)} %pad_maximum_fusion), channel_id=1, source_target_pairs={{0,8},{8,16},{16,24},{24,32},{32,40},{40,48},{48,56},{56,64},{64,7... | collective-permute-start | bytes 6291464 | tf_op jit(solution)/shard_map/ppermute | solution.py:37
  82.3 50.5 %collective-permute-start.1 = (f32[4,128,1024]{1,2,0:T(8,128)}, f32[4,128,1024]{1,2,0:T(8,128)}, u32[]{:S(2)}, u32[]{:S(2)}) collective-permute-start(f32[4,128,1024]{1,2,0:T(8,128)} %pad_maximum_fusion.1), channel_id=1, source_target_pairs={{0,248},{8,0},{16,8},{24,16},{32,24},{40,32},{48,40},{56,48},{64,5... | collective-permute-start | bytes 6291464 | tf_op jit(solution)/shard_map/ppermute | solution.py:37
  148.0 36.5 %collective-permute-start.2 = (f32[4,256,128]{1,2,0:T(8,128)}, f32[4,256,128]{1,2,0:T(8,128)}, u32[]{:S(2)}, u32[]{:S(2)}) collective-permute-start(f32[4,256,128]{1,2,0:T(8,128)} %pad_maximum_fusion.8), channel_id=1, source_target_pairs={{0,1},{1,2},{2,3},{3,4},{4,5},{5,6},{6,7},{7,0},{8,9},{9,10},{10,1... | collective-permute-start | bytes 1572872 | tf_op jit(solution)/shard_map/ppermute | solution.py:37
  150.3 38.9 %collective-permute-start.3 = (f32[4,256,128]{1,2,0:T(8,128)}, f32[4,256,128]{1,2,0:T(8,128)}, u32[]{:S(2)}, u32[]{:S(2)}) collective-permute-start(f32[4,256,128]{1,2,0:T(8,128)} %pad_maximum_fusion.9), channel_id=1, source_target_pairs={{0,7},{1,0},{2,1},{3,2},{4,3},{5,4},{6,5},{7,6},{8,15},{9,8},{10,9... | collective-permute-start | bytes 1572872 | tf_op jit(solution)/shard_map/ppermute | solution.py:37
  192.8 1.7 copy-start.20
  192.8 1.7 copy-start.21
  192.9 1.9 copy-start.22
  192.9 2.0 copy-start.23
  192.9 2.1 copy-start.12
  192.9 2.3 copy-start.14
  194.8 37.0 %collective-permute-start.4 = (f32[4,128,1024]{1,2,0:T(8,128)}, f32[4,128,1024]{1,2,0:T(8,128)}, u32[]{:S(2)}, u32[]{:S(2)}) collective-permute-start(f32[4,128,1024]{1,2,0:T(8,128)} %pad_maximum_fusion.2), channel_id=1, source_target_pairs={{0,8},{8,16},{16,24},{24,32},{32,40},{40,48},{48,56},{56,64},{64,7... | collective-permute-start | bytes 6291464 | tf_op jit(solution)/shard_map/ppermute | solution.py:37
  196.6 37.5 %collective-permute-start.5 = (f32[4,128,1024]{1,2,0:T(8,128)}, f32[4,128,1024]{1,2,0:T(8,128)}, u32[]{:S(2)}, u32[]{:S(2)}) collective-permute-start(f32[4,128,1024]{1,2,0:T(8,128)} %pad_maximum_fusion.3), channel_id=1, source_target_pairs={{0,248},{8,0},{16,8},{24,16},{32,24},{40,32},{48,40},{56,48},{64,5... | collective-permute-start | bytes 6291464 | tf_op jit(solution)/shard_map/ppermute | solution.py:37
  199.8 34.4 %copy-start.13 = (f32[1,128,1024]{1,2,0:T(8,128)S(1)}, f32[1,128,1024]{1,2,0:T(8,128)}, u32[]{:S(2)}) copy-start(f32[1,128,1024]{1,2,0:T(8,128)} %copy-done.12) | copy-start | bytes 1572868
  199.8 34.4 %copy-start.15 = (f32[1,128,1024]{1,2,0:T(8,128)S(1)}, f32[1,128,1024]{1,2,0:T(8,128)}, u32[]{:S(2)}) copy-start(f32[1,128,1024]{1,2,0:T(8,128)} %copy-done.14) | copy-start | bytes 1572868
  241.8 32.1 %collective-permute-start.6 = (f32[4,256,128]{1,2,0:T(8,128)}, f32[4,256,128]{1,2,0:T(8,128)}, u32[]{:S(2)}, u32[]{:S(2)}) collective-permute-start(f32[4,256,128]{1,2,0:T(8,128)} %pad_maximum_fusion.10), channel_id=1, source_target_pairs={{0,1},{1,2},{2,3},{3,4},{4,5},{5,6},{6,7},{7,0},{8,9},{9,10},{10,1... | collective-permute-start | bytes 1572872 | tf_op jit(solution)/shard_map/ppermute | solution.py:37
  242.7 32.8 %collective-permute-start.7 = (f32[4,256,128]{1,2,0:T(8,128)}, f32[4,256,128]{1,2,0:T(8,128)}, u32[]{:S(2)}, u32[]{:S(2)}) collective-permute-start(f32[4,256,128]{1,2,0:T(8,128)} %pad_maximum_fusion.11), channel_id=1, source_target_pairs={{0,7},{1,0},{2,1},{3,2},{4,3},{5,4},{6,5},{7,6},{8,15},{9,8},{10,9... | collective-permute-start | bytes 1572872 | tf_op jit(solution)/shard_map/ppermute | solution.py:37
  279.1 1.7 copy-start.24
  279.1 1.7 copy-start.25
  279.1 1.9 copy-start.26
  279.1 2.0 copy-start.27
  279.1 2.2 copy-start.16
  279.1 2.3 copy-start.18
  281.1 45.5 %collective-permute-start.8 = (f32[4,128,1024]{1,2,0:T(8,128)}, f32[4,128,1024]{1,2,0:T(8,128)}, u32[]{:S(2)}, u32[]{:S(2)}) collective-permute-start(f32[4,128,1024]{1,2,0:T(8,128)} %pad_maximum_fusion.4), channel_id=1, source_target_pairs={{0,8},{8,16},{16,24},{24,32},{32,40},{40,48},{48,56},{56,64},{64,7... | collective-permute-start | bytes 6291464 | tf_op jit(solution)/shard_map/ppermute | solution.py:37
  282.9 46.1 %collective-permute-start.9 = (f32[4,128,1024]{1,2,0:T(8,128)}, f32[4,128,1024]{1,2,0:T(8,128)}, u32[]{:S(2)}, u32[]{:S(2)}) collective-permute-start(f32[4,128,1024]{1,2,0:T(8,128)} %pad_maximum_fusion.5), channel_id=1, source_target_pairs={{0,248},{8,0},{16,8},{24,16},{32,24},{40,32},{48,40},{56,48},{64,5... | collective-permute-start | bytes 6291464 | tf_op jit(solution)/shard_map/ppermute | solution.py:37
  286.1 42.9 %copy-start.17 = (f32[1,128,1024]{1,2,0:T(8,128)S(1)}, f32[1,128,1024]{1,2,0:T(8,128)}, u32[]{:S(2)}) copy-start(f32[1,128,1024]{1,2,0:T(8,128)} %copy-done.16) | copy-start | bytes 1572868
  286.1 42.9 %copy-start.19 = (f32[1,128,1024]{1,2,0:T(8,128)S(1)}, f32[1,128,1024]{1,2,0:T(8,128)}, u32[]{:S(2)}) copy-start(f32[1,128,1024]{1,2,0:T(8,128)} %copy-done.18) | copy-start | bytes 1572868
  336.6 28.0 %collective-permute-start.10 = (f32[4,256,128]{1,2,0:T(8,128)}, f32[4,256,128]{1,2,0:T(8,128)}, u32[]{:S(2)}, u32[]{:S(2)}) collective-permute-start(f32[4,256,128]{1,2,0:T(8,128)} %pad_maximum_fusion.12), channel_id=1, source_target_pairs={{0,1},{1,2},{2,3},{3,4},{4,5},{5,6},{6,7},{7,0},{8,9},{9,10},{10,1... | collective-permute-start | bytes 1572872 | tf_op jit(solution)/shard_map/ppermute | solution.py:37
  337.7 28.0 %collective-permute-start.11 = (f32[4,256,128]{1,2,0:T(8,128)}, f32[4,256,128]{1,2,0:T(8,128)}, u32[]{:S(2)}, u32[]{:S(2)}) collective-permute-start(f32[4,256,128]{1,2,0:T(8,128)} %pad_maximum_fusion.13), channel_id=1, source_target_pairs={{0,7},{1,0},{2,1},{3,2},{4,3},{5,4},{6,5},{7,6},{8,15},{9,8},{10,9... | collective-permute-start | bytes 1572872 | tf_op jit(solution)/shard_map/ppermute | solution.py:37
  369.3 1.7 copy-start.8
  369.3 1.7 copy-start.9
  369.3 1.9 copy-start.10
  369.3 2.0 copy-start.11
  369.3 2.1 copy-start.4
  369.3 2.3 copy-start.6
  371.3 50.3 %collective-permute-start.12 = (f32[4,128,1024]{1,2,0:T(8,128)}, f32[4,128,1024]{1,2,0:T(8,128)}, u32[]{:S(2)}, u32[]{:S(2)}) collective-permute-start(f32[4,128,1024]{1,2,0:T(8,128)} %pad_maximum_fusion.6), channel_id=1, source_target_pairs={{0,8},{8,16},{16,24},{24,32},{32,40},{40,48},{48,56},{56,64},{64,7... | collective-permute-start | bytes 6291464 | tf_op jit(solution)/shard_map/ppermute | solution.py:37
  373.1 50.8 %collective-permute-start.13 = (f32[4,128,1024]{1,2,0:T(8,128)}, f32[4,128,1024]{1,2,0:T(8,128)}, u32[]{:S(2)}, u32[]{:S(2)}) collective-permute-start(f32[4,128,1024]{1,2,0:T(8,128)} %pad_maximum_fusion.7), channel_id=1, source_target_pairs={{0,248},{8,0},{16,8},{24,16},{32,24},{40,32},{48,40},{56,48},{64,5... | collective-permute-start | bytes 6291464 | tf_op jit(solution)/shard_map/ppermute | solution.py:37
  376.3 47.6 %copy-start.5 = (f32[1,128,1024]{1,2,0:T(8,128)S(1)}, f32[1,128,1024]{1,2,0:T(8,128)}, u32[]{:S(2)}) copy-start(f32[1,128,1024]{1,2,0:T(8,128)} %copy-done.4) | copy-start | bytes 1572868
  376.3 47.6 %copy-start.7 = (f32[1,128,1024]{1,2,0:T(8,128)S(1)}, f32[1,128,1024]{1,2,0:T(8,128)}, u32[]{:S(2)}) copy-start(f32[1,128,1024]{1,2,0:T(8,128)} %copy-done.6) | copy-start | bytes 1572868
  430.8 13.0 %collective-permute-start.14 = (f32[4,256,128]{1,2,0:T(8,128)S(1)}, f32[4,256,128]{1,2,0:T(8,128)S(1)}, u32[]{:S(2)}, u32[]{:S(2)}) collective-permute-start(f32[4,256,128]{1,2,0:T(8,128)S(1)} %pad_maximum_fusion.14), channel_id=1, source_target_pairs={{0,1},{1,2},{2,3},{3,4},{4,5},{5,6},{6,7},{7,0},{8,9},{9,10},{10,1... | collective-permute-start | bytes 1572872 | tf_op jit(solution)/shard_map/ppermute | solution.py:37
  430.9 16.4 %collective-permute-start.15 = (f32[4,256,128]{1,2,0:T(8,128)S(1)}, f32[4,256,128]{1,2,0:T(8,128)S(1)}, u32[]{:S(2)}, u32[]{:S(2)}) collective-permute-start(f32[4,256,128]{1,2,0:T(8,128)S(1)} %pad_maximum_fusion.15), channel_id=1, source_target_pairs={{0,7},{1,0},{2,1},{3,2},{4,3},{5,4},{6,5},{7,6},{8,15},{9,8},{10,9... | collective-permute-start | bytes 1572872 | tf_op jit(solution)/shard_map/ppermute | solution.py:37
Sparse Core Ops, SparseCore 0:
  41.0 25.9 all-gather.2
  68.8 51.0 all-gather.4
where the time goes:
time: 465 us; the launch traced here: 458 us
  waiting for transfers between devices  250 us (54%)
  between operations  56.2 us (12%)
  other arithmetic  52 us (11%)
  starting transfers between devices  29.8 us (6%)
  blocking collectives  24.4 us (5%)
  matrix products  24.3 us (5%)
  local copies, waits for them, and re-layouts  21.9 us (5%)
    ppermute x16, waiting for transfers between devices, from_behind(): return lax.ppermute(value, axis, pairs)  223 us
    ppermute x16, starting transfers between devices, from_behind(): return lax.ppermute(value, axis, pairs)  29.7 us
    all_gather x2, waiting for transfers between devices, gather_axes(): x = lax.all_gather(x, axis, axis=dim, tiled=True)  26.1 us
    all_to_all x1, blocking collectives, sent_to_all(): lax.all_to_all(jnp.broadcast_to(x[None], (length, *x.shape)), axis, 0, 0,...  24.4 us
    another operation x24, other arithmetic, owned_blocks(): return (jnp.stack(portions), places)  19.3 us
    dot_general x4, matrix products, local(): jnp.einsum('cji,cjk->cik', advance_factors, window, precision=lax.Precisi...  16.8 us
    add x4, other arithmetic, local(): first_rows + got_first  10.8 us
  transfers between devices with their start and end apart: 18, of which 12 were waited for; matrix products, arithmetic and copies ran while one was open for 7% of the time, Pallas kernels for 0%

commit v1 on v0

v1 whole, which is shorter than its diff:
```python
import jax
import jax.numpy as jnp
from jax import lax
from jax.experimental import pallas as pl
from jax.experimental.pallas import tpu as pltpu
from jax.sharding import PartitionSpec as P

NB = 128
CHAINS = 4
ADV = 4
ROWS = 32
COLS = 8
EACH = 32


def pack_kernel(tile, factors, out):
    lane_tiles = tile.shape[1] // NB
    for s in range(lane_tiles):
        for t in range(tile.shape[0] // NB):
            block = tile[t * NB : (t + 1) * NB, s * NB : (s + 1) * NB].T
            out[4 * s : 4 * s + 4, :EACH, t * NB : (t + 1) * NB] = block.reshape(4, EACH, NB)
    for half in range(2):
        pieces = [factors[2 * half + a, c] for a in range(2) for c in range(CHAINS)]
        piece = jnp.concatenate(pieces, axis=1)
        for d in range(half, 4 * lane_tiles, 2):
            out[d, EACH:, :] = piece


def pack(tile, factors):
    step = 256
    return pl.pallas_call(
        pack_kernel,
        grid=(tile.shape[1] // step,),
        in_specs=[
            pl.BlockSpec((256, step), lambda i: (0, i)),
            pl.BlockSpec((ADV, CHAINS, 8, 32), lambda i: (0, 0, 0, 0)),
        ],
        out_specs=pl.BlockSpec((step // EACH, EACH + 8, 256), lambda i: (i, 0, 0)),
        out_shape=jax.ShapeDtypeStruct((ROWS, EACH + 8, 256), jnp.float32),
        name="pack",
    )(tile, factors)


def spread_kernel(pieces, out):
    turned = pieces[...].reshape(256, 256).T
    for e in range(COLS):
        out[e] = turned


def spread(got):
    return pl.pallas_call(
        spread_kernel,
        grid=(1,),
        in_specs=[pl.BlockSpec((ROWS, 8, 256), lambda i: (0, EACH // 8, 0))],
        out_specs=pl.BlockSpec((COLS, 256, 256), lambda i: (0, 0, 0)),
        out_shape=jax.ShapeDtypeStruct((COLS, 256, 256), jnp.float32),
        name="spread",
    )(got)


def split(x):
    high = x.astype(jnp.bfloat16)
    return high, (x - high.astype(jnp.float32)).astype(jnp.bfloat16)


def times_factor(panel, turned_factor):
    dims = (((1,), (1,)), ((), ()))
    p_high, p_low = split(panel)
    u_high, u_low = split(turned_factor)
    both = jnp.concatenate([p_high, p_low], axis=0)
    first = lax.dot_general(both, u_high, dims, preferred_element_type=jnp.float32)
    second = lax.dot_general(p_high, u_low, dims, preferred_element_type=jnp.float32)
    return first[:EACH] + (first[EACH:] + second)


def apply_windows(panel, count, starts, core, own, other):
    def place(block):
        return lax.rem(block, count), pl.multiple_of(lax.div(block, count) * NB, NB)

    for k in range(ADV):
        is_own = core[0] == k // 2
        results = []
        for c in range(CHAINS):
            head = lax.div(starts[k, c], NB)
            p0, o0 = place(head)
            p1, o1 = place(head + 1)
            window = jnp.concatenate(
                [panel[p0, :, pl.ds(o0, NB)], panel[p1, :, pl.ds(o1, NB)]], axis=1
            )
            at = ((k % 2) * CHAINS + c) * 32
            factor = jnp.where(is_own, own[:, at : at + 32, :], other[:, at : at + 32, :])
            results.append((p0, o0, p1, o1, times_factor(window, factor.reshape(256, 256))))
        for p0, o0, p1, o1, new in results:
            panel[p0, :, pl.ds(o0, NB)] = new[:, :NB]
            panel[p1, :, pl.ds(o1, NB)] = new[:, NB:]


def swap_groups(parts):
    a0, a1, a2, a3 = parts
    axis = a0.ndim - 1
    lane = lax.broadcasted_iota(jnp.int32, a0.shape, axis)
    low = lane < 64
    even = lax.rem(lane, 64) < 32

    def roll(x, by):
        return pltpu.roll(x, by, axis)

    b0 = jnp.where(low, a0, roll(a2, 64))
    b2 = jnp.where(low, roll(a0, 64), a2)
    b1 = jnp.where(low, a1, roll(a3, 64))
    b3 = jnp.where(low, roll(a1, 64), a3)
    return (
        jnp.where(even, b0, roll(b1, 32)),
        jnp.where(even, roll(b0, 96), b1),
        jnp.where(even, b2, roll(b3, 32)),
        jnp.where(even, roll(b2, 96), b3),
    )


def row_kernel(starts, core, data, own, other, out, panel):
    panel[...] = data[...]
    apply_windows(panel, ROWS, starts, core, own, other)
    for t in range(ROWS // 4):
        for slot in range(2):
            block = panel[4 * t : 4 * t + 4, :, slot * NB : (slot + 1) * NB]
            turned = block.reshape(NB, NB).T.reshape(4, 4, 8, NB)
            parts = swap_groups([turned[:, g] for g in range(4)])
            for j in range(4):
                out[4 * t + j, 4 * slot : 4 * slot + 4] = parts[j]


def col_kernel(starts, core, data, own, other, out):
    for s in range(ROWS // 4):
        parts = swap_groups([data[4 * s + j] for j in range(4)])
        for g in range(4):
            out[:, 8 * g : 8 * g + 8, s * NB : (s + 1) * NB] = parts[g]
    apply_windows(out, COLS, starts, core, own, other)


SCALAR = pl.BlockSpec(memory_space=pltpu.SMEM)


def whole(*shape):
    return pl.BlockSpec(shape, lambda i: (0,) * len(shape))


def local(matrix, starts, factors):
    core = lax.rem(lax.axis_index("rows"), 2).reshape(1)
    packed = pack(matrix, factors)
    got = lax.all_to_all(packed, "rows", 0, 0, tiled=True)
    own = lax.all_to_all(spread(got), "cols", 0, 0, tiled=True)
    other = lax.ppermute(own, "rows", [(d, d ^ 1) for d in range(ROWS)])
    sent = pl.pallas_call(
        row_kernel,
        grid=(1,),
        in_specs=[SCALAR, SCALAR, whole(ROWS, EACH, 256)] + [whole(COLS, 256, 256)] * 2,
        out_specs=whole(ROWS, COLS, 8, NB),
        out_shape=jax.ShapeDtypeStruct((ROWS, COLS, 8, NB), jnp.float32),
        scratch_shapes=[pltpu.VMEM((ROWS, EACH, 256), jnp.float32)],
        name="row_windows",
    )(starts, core, got, own, other)
    sent = sent.reshape(ROWS * COLS, 8, NB)
    came = lax.all_to_all(sent, ("rows", "cols"), 0, 0, tiled=True)
    done = pl.pallas_call(
        col_kernel,
        grid=(1,),
        in_specs=[SCALAR, SCALAR, whole(ROWS, COLS, 8, NB)] + [whole(COLS, 256, 256)] * 2,
        out_specs=whole(COLS, EACH, 1024),
        out_shape=jax.ShapeDtypeStruct((COLS, EACH, 1024), jnp.float32),
        name="col_windows",
    )(starts, core, came.reshape(ROWS, COLS, 8, NB), own, other)
    home = lax.all_to_all(done, "cols", 0, 0, tiled=True)
    return home.reshape(256, 1024)


def solution(mesh):
    in_specs = (P("rows", "cols"), P(), P(None, None, "rows", "cols"))
    return jax.shard_map(
        local, mesh=mesh, in_specs=in_specs, out_specs=P("rows", "cols"), check_vma=False
    )
```

time: 465 us -> 161 us (0.35)
  waiting for transfers between devices: 250 us -> 4.29 us
  blocking collectives: 24.4 us -> 135 us
  between operations: 56.2 us -> 0.01 us
  other arithmetic: 52 us -> 0 us
  starting transfers between devices: 29.8 us -> 0.01 us
  matrix products: 24.3 us -> 0 us
  local copies, waits for them, and re-layouts: 21.9 us -> 0.97 us
  Pallas kernels: 0 us -> 18 us
    ppermute x16 -> x1, waiting for transfers between devices: 223 us -> 4.29 us  [local(): other = lax.ppermute(own, 'rows', [(d, d ^ 1) for d in range(ROWS)])]
    all_to_all x1 -> x4, blocking collectives: 24.4 us -> 135 us  [the longest x1 41.5 us: local(): got = lax.all_to_all(packed, 'rows', 0, 0, tiled=True)]
    ppermute x16 -> x1, starting transfers between devices: 29.7 us -> 0.01 us  [local(): other = lax.ppermute(own, 'rows', [(d, d ^ 1) for d in range(ROWS)])]
    add x16 -> x0, other arithmetic: 26.4 us -> none  [the longest x4 10.8 us: local(): first_rows + got_first]
    all_gather x2 -> x0, waiting for transfers between devices: 26.1 us -> none  [gather_axes(): x = lax.all_gather(x, axis, axis=dim, tiled=True)]
    dot_general x8 -> x0, matrix products: 24.3 us -> none  [the longest x4 16.8 us: local(): jnp.einsum('cji,cjk->cik', advance_factors, window, precision=lax.Precisi...]
    another operation x24 -> x0, other arithmetic: 19.3 us -> none  [owned_blocks(): return (jnp.stack(portions), places)]
    pallas_call x0 -> x4, Pallas kernels: none -> 18 us  [the longest x1 6.1 us: local(): pl.pallas_call(row_kernel, grid=(1,), in_specs=[SCALAR, SCALAR, whole(ROW...]
  transfers between devices with their start and end apart: 18 -> 1, of which waited for: 12 -> 1; matrix products, arithmetic and copies ran while one was open for 7% -> 0% of each run, Pallas kernels for 0% -> 0%
where the time goes in v1:
time: 161 us; the launch traced here: 158 us
  blocking collectives  135 us (84%)
  Pallas kernels  18 us (11%)
  waiting for transfers between devices  4.29 us (3%)
    all_to_all x1, blocking collectives, local(): got = lax.all_to_all(packed, 'rows', 0, 0, tiled=True)  41.5 us
    all_to_all x1, blocking collectives, local(): came = lax.all_to_all(sent, ('rows', 'cols'), 0, 0, tiled=True)  37.3 us
    all_to_all x1, blocking collectives, local(): own = lax.all_to_all(spread(got), 'cols', 0, 0, tiled=True)  34.5 us
    all_to_all x1, blocking collectives, local(): home = lax.all_to_all(done, 'cols', 0, 0, tiled=True)  21.9 us
    pallas_call x1, Pallas kernels, local(): pl.pallas_call(row_kernel, grid=(1,), in_specs=[SCALAR, SCALAR, whole(ROW...  6.1 us
    pallas_call x1, Pallas kernels, local(): pl.pallas_call(col_kernel, grid=(1,), in_specs=[SCALAR, SCALAR, whole(ROW...  5.62 us
    ppermute x1, waiting for transfers between devices, local(): other = lax.ppermute(own, 'rows', [(d, d ^ 1) for d in range(ROWS)])  4.29 us
    pallas_call x1, Pallas kernels, pack(): pl.pallas_call(pack_kernel, grid=(tile.shape[1] // step,), in_specs=[pl.B...  3.72 us
  transfers between devices with their start and end apart: 1, of which 1 were waited for; matrix products, arithmetic and copies ran while one was open for 0% of the time, Pallas kernels for 0%

profile of v1, /device:TPU:72, one launch (start us, length us, event | category | flops | bytes accessed | tf_op | source)
XLA Modules:
  0.0 158.5 jit_solution(13971915920077929763)
XLA Ops:
  0.0 3.7 %pack.1 = f32[32,40,256]{2,1,0:T(8,128)} custom-call(f32[256,1024]{1,0:T(8,128)} %tile.1, f32[4,4,8,32]{3,2,1,0:T(8,128)} %factors.1), custom_call_target="tpu_custom_call" | custom-call | tf_op jit(solution)/shard_map/pack/pallas_call | solution.py:31
  3.7 41.5 %all_to_all.20.pieces.data = f32[32,40,256]{2,1,0:T(8,128)} all-to-all(f32[32,40,256]{2,1,0:T(8,128)} %pack.1), channel_id=1, replica_groups=mesh['rows'=32,'cols'=8] {'rows'}, dimensions={0} | all-to-all | bytes 2621440 | tf_op jit(solution)/shard_map/all_to_all | solution.py:150
  45.2 2.6 %spread.1 = f32[8,256,256]{2,1,0:T(8,128)} custom-call(f32[32,40,256]{2,1,0:T(8,128)} %all_to_all.20.pieces.data), custom_call_target="tpu_custom_call" | custom-call | tf_op jit(solution)/shard_map/spread/pallas_call | solution.py:51
  47.8 34.5 %all_to_all.21.own = f32[8,256,256]{2,1,0:T(8,128)S(1)} all-to-all(f32[8,256,256]{2,1,0:T(8,128)} %spread.1), channel_id=1, replica_groups=mesh['rows'=32,'cols'=8] {'cols'}, dimensions={0} | all-to-all | bytes 4194304 | tf_op jit(solution)/shard_map/all_to_all | solution.py:151
  82.2 0.0 copy-start
  82.2 0.0 collective-permute-start
  82.2 4.3 %collective-permute-done.other = f32[8,256,256]{2,1,0:T(8,128)} collective-permute-done((f32[8,256,256]{2,1,0:T(8,128)S(1)}, f32[8,256,256]{2,1,0:T(8,128)}, u32[]{:S(2)}, u32[]{:S(2)}) %collective-permute-start) | collective-permute-done | bytes 2097184 | tf_op jit(solution)/shard_map/ppermute | solution.py:152
  86.5 0.0 copy-done
  86.5 6.1 %row_windows.1 = f32[32,8,8,128]{3,2,1,0:T(8,128)} custom-call(s32[4,4]{1,0:T(4,128)} %starts.3, s32[1]{0:T(128)} %bitcast.core, f32[32,40,256]{2,1,0:T(8,128)} %all_to_all.20.pieces.data, f32[8,256,256]{2,1,0:T(8,128)} %copy-done, f32[8,256,256]{2,1,0:T(8,128)} %collective-permute-done.other), custom_call_target="tpu_custom_call" | custom-call | tf_op jit(solution)/shard_map/row_windows/pallas_call | solution.py:153
  92.6 37.3 %all_to_all.22 = f32[256,8,128]{2,1,0:T(8,128)} all-to-all(f32[256,8,128]{2,1,0:T(8,128)} %bitcast.4), channel_id=1, replica_groups=mesh['rows'=32,'cols'=8] {'rows','cols'}, dimensions={0} | all-to-all | bytes 2097152 | tf_op jit(solution)/shard_map/all_to_all | solution.py:163
  130.0 5.6 %col_windows.1 = f32[8,32,1024]{2,1,0:T(8,128)} custom-call(s32[4,4]{1,0:T(4,128)} %starts.3, s32[1]{0:T(128)} %bitcast.core, f32[32,8,8,128]{3,2,1,0:T(8,128)} %bitcast.6, f32[8,256,256]{2,1,0:T(8,128)} %copy-done, f32[8,256,256]{2,1,0:T(8,128)} %collective-permute-done.other), custom_call_target="tpu_custom_call" | custom-call | tf_op jit(solution)/shard_map/col_windows/pallas_call | solution.py:164
  135.6 21.9 %all_to_all.23 = f32[8,32,1024]{2,1,0:T(8,128)S(1)} all-to-all(f32[8,32,1024]{2,1,0:T(8,128)} %col_windows.1), channel_id=1, replica_groups=mesh['rows'=32,'cols'=8] {'cols'}, dimensions={0} | all-to-all | bytes 2097152 | tf_op jit(solution)/shard_map/all_to_all | solution.py:172
  157.5 1.0 copy.5
Async XLA Ops:
  82.2 4.3 %copy-start = (f32[8,256,256]{2,1,0:T(8,128)}, f32[8,256,256]{2,1,0:T(8,128)S(1)}, u32[]{:S(2)}) copy-start(f32[8,256,256]{2,1,0:T(8,128)S(1)} %all_to_all.21.own) | copy-start | bytes 6291460
  82.2 4.3 %collective-permute-start = (f32[8,256,256]{2,1,0:T(8,128)S(1)}, f32[8,256,256]{2,1,0:T(8,128)}, u32[]{:S(2)}, u32[]{:S(2)}) collective-permute-start(f32[8,256,256]{2,1,0:T(8,128)S(1)} %all_to_all.21.own), channel_id=1, source_target_pairs={{0,8},{8,0},{16,24},{24,16},{32,40},{40,32},{48,56},{56,48},{64,72... | collective-permute-start | bytes 6291464 | tf_op jit(solution)/shard_map/ppermute | solution.py:152

commit v2 on v0

v2 whole, which is shorter than its diff:
```python
import jax
import jax.numpy as jnp
from jax import lax
from jax.experimental import pallas as pl
from jax.experimental.pallas import tpu as pltpu
from jax.sharding import Mesh
from jax.sharding import PartitionSpec as P


NB = 128
CHAINS = 4
ADV = 4
PLANES = 8
QUADS = 4
COLS = 8
EACH = 32
WIDE = 256


def pieces_kernel(factors, out):
    for half in range(2):
        pieces = [factors[2 * half + a, c] for a in range(2) for c in range(CHAINS)]
        piece = jnp.concatenate(pieces, axis=1)
        for d in range(half, PLANES * QUADS, 2):
            out[d] = piece


def spread_kernel(pieces, out):
    turned = pieces[...].reshape(WIDE, WIDE).T
    for e in range(COLS):
        out[e] = turned


def split(x):
    high = x.astype(jnp.bfloat16)
    return high, (x - high.astype(jnp.float32)).astype(jnp.bfloat16)


def turned_factor(k, c, core, own, other):
    at = ((k % 2) * CHAINS + c) * 32
    picked = jnp.where(core == k // 2, own[:, at : at + 32, :], other[:, at : at + 32, :])
    return split(picked.reshape(WIDE, WIDE))


def dot(a, b, b_dim):
    return lax.dot_general(a, b, (((1,), (b_dim,)), ((), ())), preferred_element_type=jnp.float32)


def row_pass(panel, first, last, starts, place, own, other):
    for k in range(ADV):
        for c in range(CHAINS):
            offset = lax.div(starts[k, c], NB) + 1 - QUADS * place[2]
            slot = (offset >= PLANES * QUADS).astype(jnp.int32)
            head = offset - PLANES * QUADS * slot

            @pl.when((head >= first) & (head <= last))
            def _():
                f_high, f_low = turned_factor(k, c, place[0], own, other)
                window = jnp.concatenate([panel[head, slot], panel[head + 1, slot]], axis=0)
                w_high, w_low = split(window)
                new = dot(f_high, w_high, 0) + (dot(f_low, w_high, 0) + dot(f_high, w_low, 0))
                panel[head, slot] = new[:NB]
                panel[head + 1, slot] = new[NB:]


def load_plane(panel, blocks, place):
    for m, block in enumerate(blocks):
        panel[(place[1] ^ m) + 1] = block[...]


def edge_kernel(starts, place, b0, b1, b2, b3, own, other, up, down, panel):
    load_plane(panel, (b0, b1, b2, b3), place)
    down[...] = panel[1]
    row_pass(panel, 1, 3, starts, place, own, other)
    up[...] = panel[4]

    @pl.when(lax.rem(place[2], PLANES // 2) == 0)
    def _():
        down[...] = panel[1]


def row_kernel(starts, place, b0, b1, b2, b3, below, above, own, other, out, panel):
    load_plane(panel, (b0, b1, b2, b3), place)
    panel[0] = below[...]
    panel[5] = above[...]

    @pl.when(place[2] == 0)
    def _():
        panel[0, 1] = below[0]

    @pl.when(place[2] == PLANES - 1)
    def _():
        panel[5, 0] = above[1]

    row_pass(panel, 0, 4, starts, place, own, other)
    out[...] = panel[1:5]


def col_kernel(starts, place, data, own, other, out):
    for q in range(QUADS):
        out[:, :, q * WIDE : (q + 1) * WIDE] = data[q]

    def spot(block):
        return lax.rem(block, COLS), pl.multiple_of(lax.div(block, COLS) * NB, NB)

    for k in range(ADV):
        results = []
        for c in range(CHAINS):
            head = lax.div(starts[k, c], NB)
            e0, o0 = spot(head)
            e1, o1 = spot(head + 1)
            window = jnp.concatenate([out[e0, :, pl.ds(o0, NB)], out[e1, :, pl.ds(o1, NB)]], axis=1)
            w_high, w_low = split(window)
            f_high, f_low = turned_factor(k, c, place[0], own, other)
            both = dot(jnp.concatenate([w_high, w_low], axis=0), f_high, 1)
            new = both[:EACH] + (both[EACH:] + dot(w_high, f_low, 1))
            results.append((e0, o0, e1, o1, new))
        for e0, o0, e1, o1, new in results:
            out[e0, :, pl.ds(o0, NB)] = new[:, :NB]
            out[e1, :, pl.ds(o1, NB)] = new[:, NB:]


SCALARS = pl.BlockSpec(memory_space=pltpu.SMEM)
VALUES = pl.BlockSpec(memory_space=pltpu.VMEM)


def kernel(body, scalars, inputs, out_shapes, scratch=()):
    outs = [jax.ShapeDtypeStruct(shape, jnp.float32) for shape in out_shapes]
    return pl.pallas_call(
        body,
        in_specs=[SCALARS] * scalars + [VALUES] * inputs,
        out_specs=[VALUES] * len(outs),
        out_shape=outs,
        scratch_shapes=[pltpu.VMEM(shape, jnp.float32) for shape in scratch],
    )


def local(matrix, starts, factors):
    z = lax.axis_index("planes")
    q = lax.axis_index("quads")
    place = jnp.stack([lax.rem(q, 2), q, z])
    tile = matrix.reshape(2, NB, QUADS * WIDE)
    quarters = [lax.dynamic_slice_in_dim(tile, (q ^ m) * WIDE, WIDE, 2) for m in range(QUADS)]
    blocks = [quarters[0]]
    for m in range(1, QUADS):
        blocks.append(lax.ppermute(quarters[m], "quads", [(i, i ^ m) for i in range(QUADS)]))
    (sent,) = kernel(pieces_kernel, 0, 1, [(PLANES * QUADS, 8, WIDE)])(factors)
    got = lax.all_to_all(sent, ("planes", "quads"), 0, 0, tiled=True)
    (sent,) = kernel(spread_kernel, 0, 1, [(COLS, WIDE, WIDE)])(got)
    own = lax.all_to_all(sent, "cols", 0, 0, tiled=True)
    other = lax.ppermute(own, "quads", [(i, i ^ 1) for i in range(QUADS)])
    panel = (QUADS + 2, 2, NB, WIDE)
    up, down = kernel(edge_kernel, 2, 6, [(2, NB, WIDE)] * 2, [panel])(
        starts, place, *blocks, own, other
    )
    below = lax.ppermute(up, "planes", [(i, (i + 1) % PLANES) for i in range(PLANES)])
    above = lax.ppermute(down, "planes", [(i, (i - 1) % PLANES) for i in range(PLANES)])
    (rows,) = kernel(row_kernel, 2, 8, [(QUADS, 2, NB, WIDE)], [panel])(
        starts, place, *blocks, below, above, own, other
    )
    rows = rows.reshape(QUADS * COLS, EACH, WIDE)
    came = lax.all_to_all(rows, ("quads", "cols"), 0, 0, tiled=True)
    came = came.reshape(QUADS, COLS, EACH, WIDE)
    (done,) = kernel(col_kernel, 2, 3, [(COLS, EACH, QUADS * WIDE)])(
        starts, place, came, own, other
    )
    home = lax.all_to_all(done, "cols", 0, 0, tiled=True)
    return home.reshape(2 * NB, QUADS * WIDE)


def solution(mesh):
    finer = Mesh(mesh.devices.reshape(PLANES, QUADS, COLS), ("planes", "quads", "cols"))
    rows = ("planes", "quads")
    in_specs = (P(rows, "cols"), P(), P(None, None, rows, "cols"))
    return jax.shard_map(
        local, mesh=finer, in_specs=in_specs, out_specs=P(rows, "cols"), check_vma=False
    )
```

time: 465 us -> 147 us (0.32)
  the two profiles are of different devices: /device:TPU:72 before, /device:TPU:1 now
where the time goes in v2:
time: 147 us
  blocking collectives  99.4 us (68%)
  Pallas kernels  19 us (13%)
  waiting for transfers between devices  16.4 us (11%)
  starting transfers between devices  7.26 us (5%)
  local copies, waits for them, and re-layouts  4.12 us (3%)
    all_to_all x1, blocking collectives, local(): own = lax.all_to_all(sent, 'cols', 0, 0, tiled=True)  33.1 us
    all_to_all x1, blocking collectives, local(): came = lax.all_to_all(rows, ('quads', 'cols'), 0, 0, tiled=True)  23.8 us
    all_to_all x1, blocking collectives, local(): got = lax.all_to_all(sent, ('planes', 'quads'), 0, 0, tiled=True)  22.7 us
    all_to_all x1, blocking collectives, local(): home = lax.all_to_all(done, 'cols', 0, 0, tiled=True)  19.9 us
    ppermute x3, waiting for transfers between devices, local(): lax.ppermute(quarters[m], 'quads', [(i, i ^ m) for i in range(QUADS)])  10.8 us
    ppermute x1, waiting for transfers between devices, local(): lax.ppermute(up, 'planes', [(i, (i + 1) % PLANES) for i in range(PLANES)])  5.6 us
    pallas_call x1, Pallas kernels, local(): kernel(row_kernel, 2, 8, [(QUADS, 2, NB, WIDE)], [panel])  5.19 us
    pallas_call x1, Pallas kernels, local(): kernel(col_kernel, 2, 3, [(COLS, EACH, QUADS * WIDE)])  5.12 us
  transfers between devices with their start and end apart: 6, of which 3 were waited for; matrix products, arithmetic and copies ran while one was open for 1% of the time, Pallas kernels for 0%

profile of v2, /device:TPU:1, one launch (start us, length us, event | category | flops | bytes accessed | tf_op | source)
XLA Modules:
  0.0 146.9 jit_solution(16358244014201191147)
XLA Ops:
  0.0 1.6 %shard_map.37 = f32[32,8,256]{2,1,0:T(8,128)} custom-call(f32[4,4,8,32]{3,2,1,0:T(8,128)} %factors.1), custom_call_target="tpu_custom_call" | custom-call | tf_op jit(solution)/shard_map/pallas_call | solution.py:147
  1.6 22.7 %all_to_all.20.pieces = f32[32,8,256]{2,1,0:T(8,128)} all-to-all(f32[32,8,256]{2,1,0:T(8,128)} %shard_map.37), channel_id=1, replica_groups=mesh['planes'=8,'quads'=4,'cols'=8] {'planes','quads'}, dimensions={0} | all-to-all | bytes 524288 | tf_op jit(solution)/shard_map/all_to_all | solution.py:148
  24.3 2.6 %shard_map.38 = f32[8,256,256]{2,1,0:T(8,128)} custom-call(f32[32,8,256]{2,1,0:T(8,128)} %all_to_all.20.pieces), custom_call_target="tpu_custom_call" | custom-call | tf_op jit(solution)/shard_map/pallas_call | solution.py:149
  26.9 0.0 copy-start.4
  26.9 33.1 %all_to_all.21.own = f32[8,256,256]{2,1,0:T(8,128)S(1)} all-to-all(f32[8,256,256]{2,1,0:T(8,128)} %shard_map.38), channel_id=1, replica_groups=mesh['planes'=8,'quads'=4,'cols'=8] {'cols'}, dimensions={0} | all-to-all | bytes 4194304 | tf_op jit(solution)/shard_map/all_to_all | solution.py:150
  59.9 0.0 copy-start
  59.9 2.4 %collective-permute-start.3 = (f32[8,256,256]{2,1,0:T(8,128)S(1)}, f32[8,256,256]{2,1,0:T(8,128)}, u32[]{:S(2)}, u32[]{:S(2)}) collective-permute-start(f32[8,256,256]{2,1,0:T(8,128)S(1)} %all_to_all.21.own), channel_id=1, source_target_pairs={{0,8},{8,0},{16,24},{24,16},{1,9},{9,1},{17,25},{25,17},{2,10},{10... | collective-permute-start | bytes 6291464 | tf_op jit(solution)/shard_map/ppermute | solution.py:151
  62.4 0.0 copy-done.4
  62.4 0.9 constant_dynamic-slice_fusion
  63.3 0.6 collective-permute-start.2
  63.9 0.9 collective-permute-start.1
  64.7 0.7 collective-permute-start
  65.4 0.6 pad_add_fusion.place
  66.1 6.1 %collective-permute-done.2.b3 = f32[2,128,256]{2,1,0:T(8,128)S(1)} collective-permute-done((f32[2,128,256]{2,1,0:T(8,128)}, f32[2,128,256]{2,1,0:T(8,128)S(1)}, u32[]{:S(2)}, u32[]{:S(2)}) %collective-permute-start.2) | collective-permute-done | bytes 262176 | tf_op jit(solution)/shard_map/ppermute | solution.py:146
  72.1 0.0 copy-start.1
  72.1 4.7 %collective-permute-done.1.b2 = f32[2,128,256]{2,1,0:T(8,128)S(1)} collective-permute-done((f32[2,128,256]{2,1,0:T(8,128)}, f32[2,128,256]{2,1,0:T(8,128)S(1)}, u32[]{:S(2)}, u32[]{:S(2)}) %collective-permute-start.1) | collective-permute-done | bytes 262176 | tf_op jit(solution)/shard_map/ppermute | solution.py:146
  76.8 0.0 copy-start.2
  76.8 0.0 collective-permute-done.b1
  76.8 0.0 copy-start.3
  76.8 0.0 collective-permute-done.3.other
  76.8 0.0 copy-done
  76.9 0.0 copy-done.1
  76.9 0.7 copy-done.2
  77.5 0.1 copy-done.3
  77.7 4.5 %shard_map.39 = (f32[2,128,256]{2,1,0:T(8,128)}, f32[2,128,256]{2,1,0:T(8,128)}) custom-call(s32[4,4]{1,0:T(4,128)} %starts.5, s32[3]{0:T(128)} %pad_add_fusion.place, f32[2,128,256]{2,1,0:T(8,128)} %get-tuple-element.12.b0, f32[2,128,256]{2,1,0:T(8,128)} %copy-done.3, f32[2,128,256]{2,1,0:T(8,128)} %copy-done.2, f32[2,128,256]{2,1,0:T(8,128)} %copy-done.1, ...), custom_call_target="tpu_custom_call" | custom-call | tf_op jit(solution)/shard_map/pallas_call | solution.py:153
  82.2 0.5 collective-permute-start.4
  82.7 2.2 %collective-permute-start.5 = (f32[2,128,256]{2,1,0:T(8,128)}, f32[2,128,256]{2,1,0:T(8,128)S(1)}, u32[]{:S(2)}, u32[]{:S(2)}) collective-permute-start(f32[2,128,256]{2,1,0:T(8,128)} %get-tuple-element.8), channel_id=1, source_target_pairs={{0,224},{32,0},{64,32},{96,64},{128,96},{160,128},{192,160},{224,1... | collective-permute-start | bytes 786440 | tf_op jit(solution)/shard_map/ppermute | solution.py:157
  84.9 5.6 %collective-permute-done.4.below = f32[2,128,256]{2,1,0:T(8,128)S(1)} collective-permute-done((f32[2,128,256]{2,1,0:T(8,128)}, f32[2,128,256]{2,1,0:T(8,128)S(1)}, u32[]{:S(2)}, u32[]{:S(2)}) %collective-permute-start.4) | collective-permute-done | bytes 262176 | tf_op jit(solution)/shard_map/ppermute | solution.py:156
  90.5 0.0 copy-start.5
  90.5 0.0 collective-permute-done.5.above
  90.5 0.7 copy-done.5
  91.2 0.0 copy-start.6
  91.2 0.7 copy-done.6
  91.9 5.2 %shard_map.40 = f32[4,2,128,256]{3,2,1,0:T(8,128)} custom-call(s32[4,4]{1,0:T(4,128)} %starts.5, s32[3]{0:T(128)} %pad_add_fusion.place, f32[2,128,256]{2,1,0:T(8,128)} %get-tuple-element.12.b0, f32[2,128,256]{2,1,0:T(8,128)} %copy-done.3, f32[2,128,256]{2,1,0:T(8,128)} %copy-done.2, f32[2,128,256]{2,1,0:T(8,128)} %copy-done.1, f32[2,128,256]{2,1,0:T(8,128)} %copy-done.5, ...), custom_call_target="tpu_custom_call" | custom-call | tf_op jit(solution)/shard_map/pallas_call | solution.py:158
  97.1 23.8 %all_to_all.22 = f32[32,32,256]{2,1,0:T(8,128)} all-to-all(f32[32,32,256]{2,1,0:T(8,128)} %bitcast.7), channel_id=1, replica_groups=mesh['planes'=8,'quads'=4,'cols'=8] {'quads','cols'}, dimensions={0} | all-to-all | bytes 2097152 | tf_op jit(solution)/shard_map/all_to_all | solution.py:162
  120.9 5.1 %shard_map.41 = f32[8,32,1024]{2,1,0:T(8,128)} custom-call(s32[4,4]{1,0:T(4,128)} %starts.5, s32[3]{0:T(128)} %pad_add_fusion.place, f32[4,8,32,256]{3,2,1,0:T(8,128)} %bitcast.9, f32[8,256,256]{2,1,0:T(8,128)} %copy-done, f32[8,256,256]{2,1,0:T(8,128)} %collective-permute-done.3.other), custom_call_target="tpu_custom_call" | custom-call | tf_op jit(solution)/shard_map/pallas_call | solution.py:164
  126.0 19.9 %all_to_all.23 = f32[8,32,1024]{2,1,0:T(8,128)S(1)} all-to-all(f32[8,32,1024]{2,1,0:T(8,128)} %shard_map.41), channel_id=1, replica_groups=mesh['planes'=8,'quads'=4,'cols'=8] {'cols'}, dimensions={0} | all-to-all | bytes 2097152 | tf_op jit(solution)/shard_map/all_to_all | solution.py:167
  145.9 1.0 copy.5
Async XLA Ops:
  26.9 35.5 %copy-start.4 = (f32[256,1024]{1,0:T(8,128)S(1)}, f32[256,1024]{1,0:T(8,128)}, u32[]{:S(2)}) copy-start(f32[256,1024]{1,0:T(8,128)} %param.3) | copy-start | bytes 3145732
  59.9 16.9 %copy-start = (f32[8,256,256]{2,1,0:T(8,128)}, f32[8,256,256]{2,1,0:T(8,128)S(1)}, u32[]{:S(2)}) copy-start(f32[8,256,256]{2,1,0:T(8,128)S(1)} %all_to_all.21.own) | copy-start | bytes 6291460
  59.9 16.9 %collective-permute-start.3 = (f32[8,256,256]{2,1,0:T(8,128)S(1)}, f32[8,256,256]{2,1,0:T(8,128)}, u32[]{:S(2)}, u32[]{:S(2)}) collective-permute-start(f32[8,256,256]{2,1,0:T(8,128)S(1)} %all_to_all.21.own), channel_id=1, source_target_pairs={{0,8},{8,0},{16,24},{24,16},{1,9},{9,1},{17,25},{25,17},{2,10},{10... | collective-permute-start | bytes 6291464 | tf_op jit(solution)/shard_map/ppermute | solution.py:151
  63.3 8.8 %collective-permute-start.2 = (f32[2,128,256]{2,1,0:T(8,128)}, f32[2,128,256]{2,1,0:T(8,128)S(1)}, u32[]{:S(2)}, u32[]{:S(2)}) collective-permute-start(f32[2,128,256]{2,1,0:T(8,128)} %get-tuple-element.9), channel_id=1, source_target_pairs={{0,24},{8,16},{16,8},{24,0},{1,25},{9,17},{17,9},{25,1},{2,26},{10... | collective-permute-start | bytes 786440 | tf_op jit(solution)/shard_map/ppermute | solution.py:146
  63.9 13.0 %collective-permute-start.1 = (f32[2,128,256]{2,1,0:T(8,128)}, f32[2,128,256]{2,1,0:T(8,128)S(1)}, u32[]{:S(2)}, u32[]{:S(2)}) collective-permute-start(f32[2,128,256]{2,1,0:T(8,128)} %get-tuple-element.10), channel_id=1, source_target_pairs={{0,16},{8,24},{16,0},{24,8},{1,17},{9,25},{17,1},{25,9},{2,18},{10... | collective-permute-start | bytes 786440 | tf_op jit(solution)/shard_map/ppermute | solution.py:146
  64.7 12.1 %collective-permute-start = (f32[2,128,256]{2,1,0:T(8,128)S(1)}, f32[2,128,256]{2,1,0:T(8,128)S(1)}, u32[]{:S(2)}, u32[]{:S(2)}) collective-permute-start(f32[2,128,256]{2,1,0:T(8,128)S(1)} %get-tuple-element.11), channel_id=1, source_target_pairs={{0,8},{8,0},{16,24},{24,16},{1,9},{9,1},{17,25},{25,17},{2,10},{10... | collective-permute-start | bytes 786440 | tf_op jit(solution)/shard_map/ppermute | solution.py:146
  72.1 4.7 %copy-start.1 = (f32[2,128,256]{2,1,0:T(8,128)}, f32[2,128,256]{2,1,0:T(8,128)S(1)}, u32[]{:S(2)}) copy-start(f32[2,128,256]{2,1,0:T(8,128)S(1)} %collective-permute-done.2.b3) | copy-start | bytes 786436
  76.8 0.7 copy-start.2
  76.8 0.8 copy-start.3
  82.2 8.3 %collective-permute-start.4 = (f32[2,128,256]{2,1,0:T(8,128)}, f32[2,128,256]{2,1,0:T(8,128)S(1)}, u32[]{:S(2)}, u32[]{:S(2)}) collective-permute-start(f32[2,128,256]{2,1,0:T(8,128)} %get-tuple-element.7), channel_id=1, source_target_pairs={{0,32},{32,64},{64,96},{96,128},{128,160},{160,192},{192,224},{224... | collective-permute-start | bytes 786440 | tf_op jit(solution)/shard_map/ppermute | solution.py:156
  82.7 7.8 %collective-permute-start.5 = (f32[2,128,256]{2,1,0:T(8,128)}, f32[2,128,256]{2,1,0:T(8,128)S(1)}, u32[]{:S(2)}, u32[]{:S(2)}) collective-permute-start(f32[2,128,256]{2,1,0:T(8,128)} %get-tuple-element.8), channel_id=1, source_target_pairs={{0,224},{32,0},{64,32},{96,64},{128,96},{160,128},{192,160},{224,1... | collective-permute-start | bytes 786440 | tf_op jit(solution)/shard_map/ppermute | solution.py:157
  90.5 0.7 copy-start.5
  91.2 0.7 copy-start.6

commit v3 on v2

--- a/solution.py
+++ b/solution.py
@@ -25,6 +25,11 @@
             out[d] = piece
 
 
+def gather_kernel(place, b0, b1, b2, b3, out):
+    for m, block in enumerate((b0, b1, b2, b3)):
+        out[place[1] ^ m] = block[...]
+
+
 def spread_kernel(pieces, out):
     turned = pieces[...].reshape(WIDE, WIDE).T
     for e in range(COLS):
@@ -46,16 +51,16 @@
     return lax.dot_general(a, b, (((1,), (b_dim,)), ((), ())), preferred_element_type=jnp.float32)
 
 
-def row_pass(panel, first, last, starts, place, own, other):
+def row_pass(panel, plane, first, last, starts, core, own, other):
     for k in range(ADV):
         for c in range(CHAINS):
-            offset = lax.div(starts[k, c], NB) + 1 - QUADS * place[2]
+            offset = lax.div(starts[k, c], NB) + 1 - QUADS * plane
             slot = (offset >= PLANES * QUADS).astype(jnp.int32)
             head = offset - PLANES * QUADS * slot
 
             @pl.when((head >= first) & (head <= last))
             def _():
-                f_high, f_low = turned_factor(k, c, place[0], own, other)
+                f_high, f_low = turned_factor(k, c, core, own, other)
                 window = jnp.concatenate([panel[head, slot], panel[head + 1, slot]], axis=0)
                 w_high, w_low = split(window)
                 new = dot(f_high, w_high, 0) + (dot(f_low, w_high, 0) + dot(f_high, w_low, 0))
@@ -63,36 +68,45 @@
                 panel[head + 1, slot] = new[NB:]
 
 
-def load_plane(panel, blocks, place):
-    for m, block in enumerate(blocks):
-        panel[(place[1] ^ m) + 1] = block[...]
+def crossing(starts, first_block):
+    found = jnp.int32(0)
+    for k in range(ADV):
+        for c in range(CHAINS):
+            head = lax.div(starts[k, c], NB) + 1
+            near = (head == first_block) | (head == first_block + PLANES * QUADS)
+            found = found | near.astype(jnp.int32)
+    return found == 1
 
 
-def edge_kernel(starts, place, b0, b1, b2, b3, own, other, up, down, panel):
-    load_plane(panel, (b0, b1, b2, b3), place)
-    down[...] = panel[1]
-    row_pass(panel, 1, 3, starts, place, own, other)
-    up[...] = panel[4]
+def row_kernel(starts, place, lower, middle, upper, own, other, out, panel, side):
+    core, plane = place[0], place[2]
+    below = lax.rem(plane + PLANES - 1, PLANES)
+    above = lax.rem(plane + 1, PLANES)
+    into = crossing(starts, QUADS * plane)
+    out_of = crossing(starts, QUADS * plane + QUADS)
+    shift_low = (plane == 0).astype(jnp.int32)
+    shift_high = (plane == PLANES - 1).astype(jnp.int32)
 
-    @pl.when(lax.rem(place[2], PLANES // 2) == 0)
+    @pl.when(into | (plane == 0))
     def _():
-        down[...] = panel[1]
+        side[1:5] = lower[...]
+        row_pass(side, below, 1, 3, starts, core, own, other)
+        panel[0, 0] = side[4, 0]
+        panel[0, 1] = side[4, 1 - shift_low]
 
+    @pl.when(out_of | (plane == PLANES - 1))
+    def _():
+        side[1:3] = upper[:2]
 
-def row_kernel(starts, place, b0, b1, b2, b3, below, above, own, other, out, panel):
-    load_plane(panel, (b0, b1, b2, b3), place)
-    panel[0] = below[...]
-    panel[5] = above[...]
+        @pl.when(lax.rem(above, PLANES // 2) == 0)
+        def _():
+            row_pass(side, above, 1, 1, starts, core, own, other)
 
-    @pl.when(place[2] == 0)
-    def _():
-        panel[0, 1] = below[0]
+        panel[5, 0] = side[1, shift_high]
+        panel[5, 1] = side[1, 1]
 
-    @pl.when(place[2] == PLANES - 1)
-    def _():
-        panel[5, 0] = above[1]
-
-    row_pass(panel, 0, 4, starts, place, own, other)
+    panel[1:5] = middle[...]
+    row_pass(panel, plane, 0, 4, starts, core, own, other)
     out[...] = panel[1:5]
 
 
@@ -146,17 +160,16 @@
         blocks.append(lax.ppermute(quarters[m], "quads", [(i, i ^ m) for i in range(QUADS)]))
     (sent,) = kernel(pieces_kernel, 0, 1, [(PLANES * QUADS, 8, WIDE)])(factors)
     got = lax.all_to_all(sent, ("planes", "quads"), 0, 0, tiled=True)
+    panel = (QUADS, 2, NB, WIDE)
+    (middle,) = kernel(gather_kernel, 1, 4, [panel])(place, *blocks)
+    lower = lax.ppermute(middle, "planes", [(i, (i + 1) % PLANES) for i in range(PLANES)])
+    upper = lax.ppermute(middle, "planes", [(i, (i - 1) % PLANES) for i in range(PLANES)])
     (sent,) = kernel(spread_kernel, 0, 1, [(COLS, WIDE, WIDE)])(got)
     own = lax.all_to_all(sent, "cols", 0, 0, tiled=True)
     other = lax.ppermute(own, "quads", [(i, i ^ 1) for i in range(QUADS)])
-    panel = (QUADS + 2, 2, NB, WIDE)
-    up, down = kernel(edge_kernel, 2, 6, [(2, NB, WIDE)] * 2, [panel])(
-        starts, place, *blocks, own, other
-    )
-    below = lax.ppermute(up, "planes", [(i, (i + 1) % PLANES) for i in range(PLANES)])
-    above = lax.ppermute(down, "planes", [(i, (i - 1) % PLANES) for i in range(PLANES)])
-    (rows,) = kernel(row_kernel, 2, 8, [(QUADS, 2, NB, WIDE)], [panel])(
-        starts, place, *blocks, below, above, own, other
+    wide = [(QUADS + 2, 2, NB, WIDE), (QUADS + 1, 2, NB, WIDE)]
+    (rows,) = kernel(row_kernel, 2, 5, [panel], wide)(
+        starts, place, lower, middle, upper, own, other
     )
     rows = rows.reshape(QUADS * COLS, EACH, WIDE)
     came = lax.all_to_all(rows, ("quads", "cols"), 0, 0, tiled=True)

time: 147 us -> 163 us (1.11)
  waiting for transfers between devices: 16.4 us -> 34.7 us
    ppermute x2, waiting for transfers between devices: 5.6 us -> 23.9 us  [the longest x1 22.6 us: local(): lax.ppermute(middle, 'planes', [(i, (i - 1) % PLANES) for i in range(PLAN...]
  transfers between devices with their start and end apart: 6 -> 6, of which waited for: 3 -> 4; matrix products, arithmetic and copies ran while one was open for 1% -> 1% of each run, Pallas kernels for 0% -> 1%
where the time goes in v3:
time: 163 us; the launch traced here: 162 us
  blocking collectives  99.7 us (61%)
  waiting for transfers between devices  34.7 us (21%)
  Pallas kernels  18.3 us (11%)
  starting transfers between devices  6.05 us (4%)
  local copies, waits for them, and re-layouts  2.67 us (2%)
    all_to_all x1, blocking collectives, local(): own = lax.all_to_all(sent, 'cols', 0, 0, tiled=True)  33.1 us
    all_to_all x1, blocking collectives, local(): came = lax.all_to_all(rows, ('quads', 'cols'), 0, 0, tiled=True)  24 us
    all_to_all x1, blocking collectives, local(): got = lax.all_to_all(sent, ('planes', 'quads'), 0, 0, tiled=True)  22.7 us
    ppermute x1, waiting for transfers between devices, local(): lax.ppermute(middle, 'planes', [(i, (i - 1) % PLANES) for i in range(PLAN...  22.6 us
    all_to_all x1, blocking collectives, local(): home = lax.all_to_all(done, 'cols', 0, 0, tiled=True)  19.9 us
    ppermute x3, waiting for transfers between devices, local(): lax.ppermute(quarters[m], 'quads', [(i, i ^ m) for i in range(QUADS)])  10.8 us
    pallas_call x1, Pallas kernels, local(): kernel(row_kernel, 2, 5, [panel], wide)  6.73 us
    pallas_call x1, Pallas kernels, local(): kernel(col_kernel, 2, 3, [(COLS, EACH, QUADS * WIDE)])  5.12 us
  transfers between devices with their start and end apart: 6, of which 4 were waited for; matrix products, arithmetic and copies ran while one was open for 1% of the time, Pallas kernels for 1%

profile of v3, /device:TPU:1, one launch (start us, length us, event | category | flops | bytes accessed | tf_op | source)
XLA Modules:
  0.0 162.0 jit_solution(255958206462505151)
XLA Ops:
  0.0 1.6 %shard_map.38 = f32[32,8,256]{2,1,0:T(8,128)} custom-call(f32[4,4,8,32]{3,2,1,0:T(8,128)} %factors.1), custom_call_target="tpu_custom_call" | custom-call | tf_op jit(solution)/shard_map/pallas_call | solution.py:161
  1.6 22.7 %all_to_all.20.pieces = f32[32,8,256]{2,1,0:T(8,128)} all-to-all(f32[32,8,256]{2,1,0:T(8,128)} %shard_map.38), channel_id=1, replica_groups=mesh['planes'=8,'quads'=4,'cols'=8] {'planes','quads'}, dimensions={0} | all-to-all | bytes 524288 | tf_op jit(solution)/shard_map/all_to_all | solution.py:162
  24.3 2.5 %shard_map.39 = f32[8,256,256]{2,1,0:T(8,128)} custom-call(f32[32,8,256]{2,1,0:T(8,128)} %all_to_all.20.pieces), custom_call_target="tpu_custom_call" | custom-call | tf_op jit(solution)/shard_map/pallas_call | solution.py:167
  26.8 0.0 copy-start.2
  26.9 33.1 %all_to_all.21.own = f32[8,256,256]{2,1,0:T(8,128)S(1)} all-to-all(f32[8,256,256]{2,1,0:T(8,128)} %shard_map.39), channel_id=1, replica_groups=mesh['planes'=8,'quads'=4,'cols'=8] {'cols'}, dimensions={0} | all-to-all | bytes 4194304 | tf_op jit(solution)/shard_map/all_to_all | solution.py:168
  59.9 0.0 copy-start
  59.9 2.4 %collective-permute-start.5 = (f32[8,256,256]{2,1,0:T(8,128)S(1)}, f32[8,256,256]{2,1,0:T(8,128)}, u32[]{:S(2)}, u32[]{:S(2)}) collective-permute-start(f32[8,256,256]{2,1,0:T(8,128)S(1)} %all_to_all.21.own), channel_id=1, source_target_pairs={{0,8},{8,0},{16,24},{24,16},{1,9},{9,1},{17,25},{25,17},{2,10},{10... | collective-permute-start | bytes 6291464 | tf_op jit(solution)/shard_map/ppermute | solution.py:169
  62.4 0.0 copy-done.2
  62.4 0.9 constant_dynamic-slice_fusion
  63.3 0.6 collective-permute-start.2
  63.9 0.9 collective-permute-start.1
  64.7 0.7 collective-permute-start
  65.4 0.6 pad_add_fusion.place
  66.1 6.0 %collective-permute-done.2.b3 = f32[2,128,256]{2,1,0:T(8,128)S(1)} collective-permute-done((f32[2,128,256]{2,1,0:T(8,128)}, f32[2,128,256]{2,1,0:T(8,128)S(1)}, u32[]{:S(2)}, u32[]{:S(2)}) %collective-permute-start.2) | collective-permute-done | bytes 262176 | tf_op jit(solution)/shard_map/ppermute | solution.py:160
  72.1 0.0 copy-start.3
  72.1 4.8 %collective-permute-done.1.b2 = f32[2,128,256]{2,1,0:T(8,128)S(1)} collective-permute-done((f32[2,128,256]{2,1,0:T(8,128)}, f32[2,128,256]{2,1,0:T(8,128)S(1)}, u32[]{:S(2)}, u32[]{:S(2)}) %collective-permute-start.1) | collective-permute-done | bytes 262176 | tf_op jit(solution)/shard_map/ppermute | solution.py:160
  76.8 0.0 copy-start.4
  76.9 0.0 collective-permute-done.b1
  76.9 0.0 copy-start.5
  76.9 0.0 copy-done.3
  76.9 0.7 copy-done.4
  77.5 0.1 copy-done.5
  77.7 2.2 %shard_map.37.middle = f32[4,2,128,256]{3,2,1,0:T(8,128)} custom-call(s32[3]{0:T(128)} %pad_add_fusion.place, f32[2,128,256]{2,1,0:T(8,128)} %get-tuple-element.8.b0, f32[2,128,256]{2,1,0:T(8,128)} %copy-done.5, f32[2,128,256]{2,1,0:T(8,128)} %copy-done.4, f32[2,128,256]{2,1,0:T(8,128)} %copy-done.3), custom_call_target="tpu_custom_call" | custom-call | tf_op jit(solution)/shard_map/pallas_call | solution.py:164
  79.9 0.0 copy-done
  79.9 0.4 collective-permute-start.4
  80.3 1.1 collective-permute-start.3
  81.4 22.6 %collective-permute-done.4.upper = f32[4,2,128,256]{3,2,1,0:T(8,128)S(1)} collective-permute-done((f32[4,2,128,256]{3,2,1,0:T(8,128)}, f32[4,2,128,256]{3,2,1,0:T(8,128)S(1)}, u32[]{:S(2)}, u32[]{:S(2)}) %collective-permute-start.4) | collective-permute-done | bytes 1048608 | tf_op jit(solution)/shard_map/ppermute | solution.py:166
  104.0 0.0 copy-start.1
  104.0 1.3 collective-permute-done.3.lower
  105.3 0.0 collective-permute-done.5.other
  105.3 0.0 copy-done.1
  105.3 6.7 %shard_map.40 = f32[4,2,128,256]{3,2,1,0:T(8,128)} custom-call(s32[4,4]{1,0:T(4,128)} %starts.3, s32[3]{0:T(128)} %pad_add_fusion.place, f32[4,2,128,256]{3,2,1,0:T(8,128)} %collective-permute-done.3.lower, f32[4,2,128,256]{3,2,1,0:T(8,128)} %shard_map.37.middle, f32[4,2,128,256]{3,2,1,0:T(8,128)} %copy-done.1, f32[8,256,256]{2,1,0:T(8,128)} %copy-done, ...), custom_call_target="tpu_custom_call" | custom-call | tf_op jit(solution)/shard_map/pallas_call | solution.py:171
  112.0 24.0 %all_to_all.22 = f32[32,32,256]{2,1,0:T(8,128)} all-to-all(f32[32,32,256]{2,1,0:T(8,128)} %bitcast.7), channel_id=1, replica_groups=mesh['planes'=8,'quads'=4,'cols'=8] {'quads','cols'}, dimensions={0} | all-to-all | bytes 2097152 | tf_op jit(solution)/shard_map/all_to_all | solution.py:175
  136.0 5.1 %shard_map.41 = f32[8,32,1024]{2,1,0:T(8,128)} custom-call(s32[4,4]{1,0:T(4,128)} %starts.3, s32[3]{0:T(128)} %pad_add_fusion.place, f32[4,8,32,256]{3,2,1,0:T(8,128)} %bitcast.9, f32[8,256,256]{2,1,0:T(8,128)} %copy-done, f32[8,256,256]{2,1,0:T(8,128)} %collective-permute-done.5.other), custom_call_target="tpu_custom_call" | custom-call | tf_op jit(solution)/shard_map/pallas_call | solution.py:177
  141.1 19.9 %all_to_all.23 = f32[8,32,1024]{2,1,0:T(8,128)S(1)} all-to-all(f32[8,32,1024]{2,1,0:T(8,128)} %shard_map.41), channel_id=1, replica_groups=mesh['planes'=8,'quads'=4,'cols'=8] {'cols'}, dimensions={0} | all-to-all | bytes 2097152 | tf_op jit(solution)/shard_map/all_to_all | solution.py:180
  161.1 1.0 copy.5
Async XLA Ops:
  26.8 35.5 %copy-start.2 = (f32[256,1024]{1,0:T(8,128)S(1)}, f32[256,1024]{1,0:T(8,128)}, u32[]{:S(2)}) copy-start(f32[256,1024]{1,0:T(8,128)} %param.3) | copy-start | bytes 3145732
  59.9 20.0 %copy-start = (f32[8,256,256]{2,1,0:T(8,128)}, f32[8,256,256]{2,1,0:T(8,128)S(1)}, u32[]{:S(2)}) copy-start(f32[8,256,256]{2,1,0:T(8,128)S(1)} %all_to_all.21.own) | copy-start | bytes 6291460
  59.9 45.3 %collective-permute-start.5 = (f32[8,256,256]{2,1,0:T(8,128)S(1)}, f32[8,256,256]{2,1,0:T(8,128)}, u32[]{:S(2)}, u32[]{:S(2)}) collective-permute-start(f32[8,256,256]{2,1,0:T(8,128)S(1)} %all_to_all.21.own), channel_id=1, source_target_pairs={{0,8},{8,0},{16,24},{24,16},{1,9},{9,1},{17,25},{25,17},{2,10},{10... | collective-permute-start | bytes 6291464 | tf_op jit(solution)/shard_map/ppermute | solution.py:169
  63.3 8.8 %collective-permute-start.2 = (f32[2,128,256]{2,1,0:T(8,128)}, f32[2,128,256]{2,1,0:T(8,128)S(1)}, u32[]{:S(2)}, u32[]{:S(2)}) collective-permute-start(f32[2,128,256]{2,1,0:T(8,128)} %get-tuple-element.5), channel_id=1, source_target_pairs={{0,24},{8,16},{16,8},{24,0},{1,25},{9,17},{17,9},{25,1},{2,26},{10... | collective-permute-start | bytes 786440 | tf_op jit(solution)/shard_map/ppermute | solution.py:160
  63.9 13.0 %collective-permute-start.1 = (f32[2,128,256]{2,1,0:T(8,128)}, f32[2,128,256]{2,1,0:T(8,128)S(1)}, u32[]{:S(2)}, u32[]{:S(2)}) collective-permute-start(f32[2,128,256]{2,1,0:T(8,128)} %get-tuple-element.6), channel_id=1, source_target_pairs={{0,16},{8,24},{16,0},{24,8},{1,17},{9,25},{17,1},{25,9},{2,18},{10... | collective-permute-start | bytes 786440 | tf_op jit(solution)/shard_map/ppermute | solution.py:160
  64.7 12.1 %collective-permute-start = (f32[2,128,256]{2,1,0:T(8,128)S(1)}, f32[2,128,256]{2,1,0:T(8,128)S(1)}, u32[]{:S(2)}, u32[]{:S(2)}) collective-permute-start(f32[2,128,256]{2,1,0:T(8,128)S(1)} %get-tuple-element.7), channel_id=1, source_target_pairs={{0,8},{8,0},{16,24},{24,16},{1,9},{9,1},{17,25},{25,17},{2,10},{10... | collective-permute-start | bytes 786440 | tf_op jit(solution)/shard_map/ppermute | solution.py:160
  72.1 4.8 %copy-start.3 = (f32[2,128,256]{2,1,0:T(8,128)}, f32[2,128,256]{2,1,0:T(8,128)S(1)}, u32[]{:S(2)}) copy-start(f32[2,128,256]{2,1,0:T(8,128)S(1)} %collective-permute-done.2.b3) | copy-start | bytes 786436
  76.8 0.7 copy-start.4
  76.9 0.8 copy-start.5
  79.9 24.1 %collective-permute-start.4 = (f32[4,2,128,256]{3,2,1,0:T(8,128)}, f32[4,2,128,256]{3,2,1,0:T(8,128)S(1)}, u32[]{:S(2)}, u32[]{:S(2)}) collective-permute-start(f32[4,2,128,256]{3,2,1,0:T(8,128)} %shard_map.37.middle), channel_id=1, source_target_pairs={{0,224},{32,0},{64,32},{96,64},{128,96},{160,128},{192,160},{224,1... | collective-permute-start | bytes 3145736 | tf_op jit(solution)/shard_map/ppermute | solution.py:166
  80.3 25.0 %collective-permute-start.3 = (f32[4,2,128,256]{3,2,1,0:T(8,128)}, f32[4,2,128,256]{3,2,1,0:T(8,128)}, u32[]{:S(2)}, u32[]{:S(2)}) collective-permute-start(f32[4,2,128,256]{3,2,1,0:T(8,128)} %shard_map.37.middle), channel_id=1, source_target_pairs={{0,32},{32,64},{64,96},{96,128},{128,160},{160,192},{192,224},{224... | collective-permute-start | bytes 3145736 | tf_op jit(solution)/shard_map/ppermute | solution.py:165
  104.0 1.3 copy-start.1
